TPU v7x, 128 devices: a whole 4x4x4 slice. The times are simulated.
128 devices in a mesh: band: 32 (over y, x_hi, z), grid: 4 (over x_lo, core).
Axes of the slice: x: 4 (x_hi: 2, x_lo: 2; x = x_hi * 2 + x_lo), y: 4, z: 4, core: 2. Of those that a mesh axis runs over, the one named last changes fastest.
Arguments:
- orbitals: float32 [96, 64, 4096], P('band', 'grid'), may hold values from -6 to 6
- pair_mask: int32 [96, 96], replicated, may hold values from 0 to 1, as said below
Outputs:
- exchange_term: float32 [96, 64, 4096], P('band', 'grid')
Inputs may be any that keep to these rules, and one draw needn't show every extreme that they name: pair_mask is symmetric; entries outside the candidate pairs of every block (and their transposes) are 0; each block has at most 12 candidate pairs with mask 1, and some block has exactly 12.
All inputs are finite; a program needn't handle non-finite values.
Results may differ from a plain program's by a relative error of at most 0.00027.
Values sent between devices are 32-bit elements; how exact they have to be, the bound alone decides.
A program may use at most 64 MiB of HBM per device.

v0:
```python
import math
import jax
import jax.numpy as jnp
import numpy as np
from jax import lax
from jax.sharding import PartitionSpec as P

NG = 64
ORB_DEV = 3
REACH = 2
NCAND = 24
CAP = 12
MIXING = 0.25
BOX_LENGTH = 16.0
EXACT_PRECISION = lax.Precision.HIGHEST
turn_pairs = 4


def shifted(block, axis, distance):
    devices = range(lax.axis_size(axis))
    route = [((i - distance) % len(devices), i) for i in devices]
    return lax.ppermute(block, axis, route)


def pair_table():
    entries = []
    for distance in range(REACH + 1):
        for leading_orbital in range(ORB_DEV):
            for second_orb in range(ORB_DEV):
                if distance > 0 or leading_orbital <= second_orb:
                    entries.append((leading_orbital, distance, second_orb))
    return np.array(entries, dtype=np.int32)


def dft_tables(length):
    positions = jnp.arange(length, dtype=jnp.int32)
    product_mod = positions[:, None] * positions[None, :] % length
    angles = product_mod.astype(jnp.float32) * (2.0 * math.pi / length)
    return (jnp.cos(angles), jnp.sin(angles))


def rotate_parts(values_in):
    half_width = values_in.shape[-1] // 2
    return jnp.concatenate([values_in[..., half_width:], -values_in[..., :half_width]], axis=-1)


def transform_axis(values_in, tables, formula, sweep_direction):
    cosine_table, sine_table = tables
    direct_part = jnp.einsum(formula, cosine_table, values_in, precision=EXACT_PRECISION)
    crossed_part = jnp.einsum(formula, sine_table, values_in, precision=EXACT_PRECISION)
    return direct_part + sweep_direction * rotate_parts(crossed_part)


def signed_frequency(positions):
    return jnp.where(positions < NG // 2, positions, positions - NG)


def coulomb_values(squared):
    safe_values = jnp.maximum(squared, 1).astype(jnp.float32)
    return jnp.where(squared > 0, BOX_LENGTH * BOX_LENGTH / math.pi / safe_values, 0.0)


def solve_poisson(density, tables, kernel_pair, z_tables):
    count_pairs = density.shape[0]
    planes = density.shape[1]
    cubes = density.reshape(count_pairs, planes, NG, NG)
    joined = jnp.concatenate([cubes[0::2], cubes[1::2]], axis=-1)
    spectrum = jnp.einsum("pxyz,zk->pxyk", joined, z_tables[0], precision=EXACT_PRECISION)
    spectrum = transform_axis(spectrum, tables, "ky,pxyc->pxkc", 1.0)
    columns = lax.all_to_all(spectrum, "grid", split_axis=2, concat_axis=1, tiled=True)
    columns = transform_axis(columns, tables, "kx,pxyc->pkyc", 1.0)
    columns = columns * kernel_pair[None]
    columns = transform_axis(columns, tables, "kx,pxyc->pkyc", -1.0)
    returned = lax.all_to_all(columns, "grid", split_axis=1, concat_axis=2, tiled=True)
    returned = transform_axis(returned, tables, "ky,pxyc->pxkc", -1.0)
    fields = jnp.einsum("pxyc,ck->pxyk", returned, z_tables[2], precision=EXACT_PRECISION)
    potential = jnp.stack([fields[..., :NG], fields[..., NG:]], axis=1)
    return potential.reshape(count_pairs, planes, NG * NG)


def local(orbitals, pair_mask):
    orb_count, planes, cells = orbitals.shape
    groups = lax.axis_size("band")
    band_index = lax.axis_index("band")
    grid_index = lax.axis_index("grid")
    visits = [orbitals]
    for distance in range(1, REACH + 1):
        visits.append(shifted(orbitals, "band", -distance))
    flat_count = (REACH + 1) * orb_count
    flat_visiting = jnp.stack(visits).reshape(flat_count, planes, cells)
    pair_list = pair_table()
    first_ids = jnp.asarray(pair_list[:, 0])
    offsets = jnp.asarray(pair_list[:, 1])
    second_ids = jnp.asarray(pair_list[:, 2])
    row_ids = band_index * ORB_DEV + first_ids
    col_ids = (band_index + offsets) % groups * ORB_DEV + second_ids
    live_flags = pair_mask[row_ids, col_ids]
    sort_keys = (1 - live_flags) * NCAND + jnp.arange(NCAND, dtype=jnp.int32)
    live_order = jnp.argsort(sort_keys)[:CAP]
    first_ids = first_ids[live_order]
    offsets = offsets[live_order]
    second_ids = second_ids[live_order]
    live_flags = live_flags[live_order]
    padding = -first_ids.shape[0] % turn_pairs

    def padded(values_in):
        return jnp.concatenate([values_in, jnp.zeros((padding,), jnp.int32)])

    first_ids = padded(first_ids)
    offsets = padded(offsets)
    second_ids = padded(second_ids)
    live_flags = padded(live_flags)
    slot_ids = offsets * ORB_DEV + second_ids
    weights = live_flags.astype(jnp.float32)
    self_flags = 1.0 - ((offsets == 0) & (first_ids == second_ids)).astype(jnp.float32)
    turns = first_ids.shape[0] // turn_pairs
    tables = dft_tables(NG)
    cosine_table, sine_table = tables
    forward_complex = jnp.block([[cosine_table, -sine_table], [sine_table, cosine_table]])
    forward_real = jnp.concatenate([cosine_table, -sine_table], axis=1)
    inverse_complex = jnp.block([[cosine_table, sine_table], [-sine_table, cosine_table]])
    inverse_real = jnp.concatenate([cosine_table, -sine_table], axis=0)
    z_tables = (forward_complex, forward_real, inverse_complex, inverse_real)
    waves_first = signed_frequency(jnp.arange(NG, dtype=jnp.int32))[:, None, None]
    waves_second = signed_frequency(grid_index * planes + jnp.arange(planes, dtype=jnp.int32))[
        None, :, None
    ]
    waves_third = signed_frequency(jnp.arange(NG, dtype=jnp.int32))[None, None, :]
    kernel = coulomb_values(
        waves_first * waves_first + waves_second * waves_second + waves_third * waves_third
    ) / float(NG**3)
    kernel_pair = jnp.concatenate([kernel, kernel], axis=-1)

    def one_turn(totals, turn_input):
        owned_total, visit_total = totals
        first_turn, slot_turn, weight_turn, self_turn = turn_input
        leading_orbital = orbitals[first_turn]
        second_orb = flat_visiting[slot_turn]
        potential = solve_poisson(leading_orbital * second_orb, tables, kernel_pair, z_tables)
        weighted_density = potential * weight_turn[:, None, None]
        owner_hot = (first_turn[:, None] == jnp.arange(orb_count, dtype=jnp.int32)[None, :]).astype(
            jnp.float32
        )
        visit_onehot_mask = (
            slot_turn[:, None] == jnp.arange(flat_count, dtype=jnp.int32)[None, :]
        ).astype(jnp.float32) * self_turn[:, None]
        owned_total = owned_total + jnp.einsum(
            "pa,pxc->axc", owner_hot, weighted_density * second_orb, precision=EXACT_PRECISION
        )
        visit_total = visit_total + jnp.einsum(
            "sq,swt->qwt",
            visit_onehot_mask,
            weighted_density * leading_orbital,
            precision=EXACT_PRECISION,
        )
        return ((owned_total, visit_total), None)

    start_totals = (
        jnp.zeros((orb_count, planes, cells), jnp.float32),
        jnp.zeros((flat_count, planes, cells), jnp.float32),
    )
    turn_inputs = (
        first_ids.reshape(turns, turn_pairs),
        slot_ids.reshape(turns, turn_pairs),
        weights.reshape(turns, turn_pairs),
        self_flags.reshape(turns, turn_pairs),
    )
    (owned_total, visit_total), discarded_value = lax.scan(one_turn, start_totals, turn_inputs)
    visit_total = visit_total.reshape(REACH + 1, orb_count, planes, cells)
    owned = owned_total + visit_total[0]
    for distance in range(1, REACH + 1):
        owned = owned + shifted(visit_total[distance], "band", distance)
    return -MIXING * owned


def solution(mesh):
    return jax.shard_map(
        local,
        mesh=mesh,
        in_specs=(P("band", "grid", None), P()),
        out_specs=P("band", "grid", None),
        check_vma=False,
    )
```

profile of v0, /device:TPU:0, one launch (start us, length us, event | category | flops | bytes accessed | tf_op | source)
XLA Modules:
  0.0 318.8 jit_solution(15074602083450062132)
XLA Ops:
  0.0 8.9 %collective-permute-start.1 = (f32[3,16,4096]{2,1,0:T(8,128)}, f32[3,16,4096]{2,1,0:T(8,128)S(1)}, u32[]{:S(2)}, u32[]{:S(2)}) collective-permute-start(f32[3,16,4096]{2,1,0:T(8,128)} %param.7), channel_id=1, source_target_pairs={{8,0},{12,4},{16,8},{20,12},{24,16},{28,20},{32,24},{36,28},{40,32... | collective-permute-start | bytes 2359304 | tf_op jit(solution)/shard_map/ppermute | solution.py:22
  11.1 1.6 sort.17
  19.6 7.6 %collective-permute-done.1 = f32[3,16,4096]{2,1,0:T(8,128)S(1)} collective-permute-done((f32[3,16,4096]{2,1,0:T(8,128)}, f32[3,16,4096]{2,1,0:T(8,128)S(1)}, u32[]{:S(2)}, u32[]{:S(2)}) %collective-permute-start.1) | collective-permute-done | bytes 786464 | tf_op jit(solution)/shard_map/ppermute | solution.py:22
  27.2 16.1 %collective-permute-done = f32[3,16,4096]{2,1,0:T(8,128)S(1)} collective-permute-done((f32[3,16,4096]{2,1,0:T(8,128)}, f32[3,16,4096]{2,1,0:T(8,128)S(1)}, u32[]{:S(2)}, u32[]{:S(2)}) %collective-permute-start) | collective-permute-done | bytes 786464 | tf_op jit(solution)/shard_map/ppermute | solution.py:22
  43.3 1.7 pad_maximum_fusion.1
  44.9 226.3 %while.14 = (s32[]{:T(128)}, f32[3,16,4096]{2,0,1:T(4,128)}, f32[9,16,4096]{2,0,1:T(8,128)}, s32[3,4]{1,0:T(4,128)S(1)}, f32[3,16,4096]{2,1,0:T(8,128)S(1)}, /*i...) while((s32[]{:T(128)}, f32[3,16,4096]{2,0,1:T(4,128)}, ...), condition=%wide.region_2.3_spmd.clone.clone, body=%wide.region_1.2_spmd.clone.clone.sunk | while | flops 2460682240 | bytes 111813288 | solution.py:168
  45.6 2.3 gather_fusion.1
  48.0 2.2 mul.862
  50.2 1.7 fusion.196
  56.6 16.9 %all_to_all.48 = f32[2,16,64,128]{3,1,0,2:T(8,128)S(1)} all-to-all(f32[2,16,64,128]{3,1,0,2:T(8,128)S(1)} %copy.52), channel_id=1, replica_groups=mesh['band'=32,'grid'=4] {'grid'}, dimensions={2} | all-to-all | bytes 2097152 | tf_op jit(solution)/shard_map/while/body/eval_jaxpr/all_to_all | solution.py:70
  75.8 1.5 fusion.201
  80.4 1.6 copy.54
  81.9 3.5 %all-to-all-start.1 = ((f32[2,64,16,128]{3,2,0,1:T(8,128)}), f32[2,64,16,128]{3,2,0,1:T(8,128)S(1)}, u32[]{:S(2)}, u32[]{:S(2)}) async-start(f32[2,64,16,128]{3,2,0,1:T(8,128)} %copy.54), calls=%async_computation.1 | async-start | bytes 2097152 | tf_op jit(solution)/shard_map/while/body/eval_jaxpr/all_to_all | solution.py:74
  85.5 14.4 %all-to-all-done.1 = f32[2,64,16,128]{3,2,0,1:T(8,128)S(1)} async-done(((f32[2,64,16,128]{3,2,0,1:T(8,128)}), f32[2,64,16,128]{3,2,0,1:T(8,128)S(1)}, u32[]{:S(2)}, u32[]{:S(2)}) %all-to-all-start.1) | async-done | bytes 1048608 | tf_op jit(solution)/shard_map/while/body/eval_jaxpr/all_to_all | solution.py:74
  104.6 1.5 copy.56
  106.2 2.1 reshape.255
  109.5 2.5 convolution_add_fusion.4
  112.0 6.4 %convolution_add_fusion.5 = f32[9,16,4096]{2,0,1:T(8,128)S(1)} fusion(f32[9,16,4096]{2,0,1:T(8,128)S(1)} %copy-done.1, pred[]{:T(512)S(6)} %compare.9, f32[4,16,4096]{2,1,0:T(8,128)S(1)} %get-tuple-element.342, f32[4]{0:T(128)S(1)} %get-tuple-element.343, s32[4]{0:T(128)S(1)} %get-tuple-element.344), kind=kOutput, calls=%fused_computation.9.clone.1 | convolution fusion | flops 29491272 | bytes 5767201 | tf_op jit(solution)/shard_map/while/body/eval_jaxpr/sq,swt->qwt/dot_general | solution.py:150
  118.4 1.9 copy-done.2
  121.0 2.3 gather_fusion.1
  123.4 2.2 mul.862
  125.7 1.7 fusion.196
  132.0 16.9 %all_to_all.48 = f32[2,16,64,128]{3,1,0,2:T(8,128)S(1)} all-to-all(f32[2,16,64,128]{3,1,0,2:T(8,128)S(1)} %copy.52), channel_id=1, replica_groups=mesh['band'=32,'grid'=4] {'grid'}, dimensions={2} | all-to-all | bytes 2097152 | tf_op jit(solution)/shard_map/while/body/eval_jaxpr/all_to_all | solution.py:70
  151.2 1.5 fusion.201
  155.8 1.6 copy.54
  157.4 3.5 %all-to-all-start.1 = ((f32[2,64,16,128]{3,2,0,1:T(8,128)}), f32[2,64,16,128]{3,2,0,1:T(8,128)S(1)}, u32[]{:S(2)}, u32[]{:S(2)}) async-start(f32[2,64,16,128]{3,2,0,1:T(8,128)} %copy.54), calls=%async_computation.1 | async-start | bytes 2097152 | tf_op jit(solution)/shard_map/while/body/eval_jaxpr/all_to_all | solution.py:74
  160.9 14.4 %all-to-all-done.1 = f32[2,64,16,128]{3,2,0,1:T(8,128)S(1)} async-done(((f32[2,64,16,128]{3,2,0,1:T(8,128)}), f32[2,64,16,128]{3,2,0,1:T(8,128)S(1)}, u32[]{:S(2)}, u32[]{:S(2)}) %all-to-all-start.1) | async-done | bytes 1048608 | tf_op jit(solution)/shard_map/while/body/eval_jaxpr/all_to_all | solution.py:74
  180.1 1.5 copy.56
  181.6 2.1 reshape.255
  185.0 2.5 convolution_add_fusion.4
  187.4 6.4 %convolution_add_fusion.5 = f32[9,16,4096]{2,0,1:T(8,128)S(1)} fusion(f32[9,16,4096]{2,0,1:T(8,128)S(1)} %copy-done.1, pred[]{:T(512)S(6)} %compare.9, f32[4,16,4096]{2,1,0:T(8,128)S(1)} %get-tuple-element.342, f32[4]{0:T(128)S(1)} %get-tuple-element.343, s32[4]{0:T(128)S(1)} %get-tuple-element.344), kind=kOutput, calls=%fused_computation.9.clone.1 | convolution fusion | flops 29491272 | bytes 5767201 | tf_op jit(solution)/shard_map/while/body/eval_jaxpr/sq,swt->qwt/dot_general | solution.py:150
  193.9 1.9 copy-done.2
  196.5 2.3 gather_fusion.1
  198.9 2.2 mul.862
  201.1 1.7 fusion.196
  207.5 16.9 %all_to_all.48 = f32[2,16,64,128]{3,1,0,2:T(8,128)S(1)} all-to-all(f32[2,16,64,128]{3,1,0,2:T(8,128)S(1)} %copy.52), channel_id=1, replica_groups=mesh['band'=32,'grid'=4] {'grid'}, dimensions={2} | all-to-all | bytes 2097152 | tf_op jit(solution)/shard_map/while/body/eval_jaxpr/all_to_all | solution.py:70
  226.7 1.5 fusion.201
  231.2 1.6 copy.54
  232.8 3.5 %all-to-all-start.1 = ((f32[2,64,16,128]{3,2,0,1:T(8,128)}), f32[2,64,16,128]{3,2,0,1:T(8,128)S(1)}, u32[]{:S(2)}, u32[]{:S(2)}) async-start(f32[2,64,16,128]{3,2,0,1:T(8,128)} %copy.54), calls=%async_computation.1 | async-start | bytes 2097152 | tf_op jit(solution)/shard_map/while/body/eval_jaxpr/all_to_all | solution.py:74
  236.4 14.4 %all-to-all-done.1 = f32[2,64,16,128]{3,2,0,1:T(8,128)S(1)} async-done(((f32[2,64,16,128]{3,2,0,1:T(8,128)}), f32[2,64,16,128]{3,2,0,1:T(8,128)S(1)}, u32[]{:S(2)}, u32[]{:S(2)}) %all-to-all-start.1) | async-done | bytes 1048608 | tf_op jit(solution)/shard_map/while/body/eval_jaxpr/all_to_all | solution.py:74
  257.0 2.1 reshape.255
  260.4 2.5 convolution_add_fusion.4
  262.9 6.4 %convolution_add_fusion.5 = f32[9,16,4096]{2,0,1:T(8,128)S(1)} fusion(f32[9,16,4096]{2,0,1:T(8,128)S(1)} %copy-done.1, pred[]{:T(512)S(6)} %compare.9, f32[4,16,4096]{2,1,0:T(8,128)S(1)} %get-tuple-element.342, f32[4]{0:T(128)S(1)} %get-tuple-element.343, s32[4]{0:T(128)S(1)} %get-tuple-element.344), kind=kOutput, calls=%fused_computation.9.clone.1 | convolution fusion | flops 29491272 | bytes 5767201 | tf_op jit(solution)/shard_map/while/body/eval_jaxpr/sq,swt->qwt/dot_general | solution.py:150
  269.3 1.9 copy-done.2
  271.2 3.6 %copy.30 = f32[9,16,4096]{2,1,0:T(8,128)S(1)} copy(f32[9,16,4096]{2,0,1:T(8,128)} %get-tuple-element.394) | data formatting | bytes 4718592 | tf_op jit(solution)/shard_map/while | solution.py:168
  275.0 2.2 collective-permute-start.2
  277.2 23.2 %collective-permute-done.3 = f32[3,16,4096]{2,1,0:T(8,128)S(1)} collective-permute-done((f32[3,16,4096]{2,1,0:T(8,128)S(1)}, f32[3,16,4096]{2,1,0:T(8,128)S(1)}, u32[]{:S(2)}, u32[]{:S(2)}) %collective-permute-start.3) | collective-permute-done | bytes 786464 | tf_op jit(solution)/shard_map/ppermute | solution.py:22
  300.4 16.9 %collective-permute-done.2 = f32[3,16,4096]{2,1,0:T(8,128)S(1)} collective-permute-done((f32[3,16,4096]{2,1,0:T(8,128)S(1)}, f32[3,16,4096]{2,1,0:T(8,128)S(1)}, u32[]{:S(2)}, u32[]{:S(2)}) %collective-permute-start.2) | collective-permute-done | bytes 786464 | tf_op jit(solution)/shard_map/ppermute | solution.py:22
  (152 shorter events, 62.2 us)
Async XLA Ops:
  0.0 10.3 %copy-start = (s32[96,96]{1,0:T(8,128)S(1)}, s32[96,96]{1,0:T(8,128)}, u32[]{:S(2)}) copy-start(s32[96,96]{1,0:T(8,128)} %param.8) | copy-start | bytes 110596
  0.0 43.3 %copy-start.3 = (f32[3,16,4096]{2,1,0:T(8,128)S(1)}, f32[3,16,4096]{2,1,0:T(8,128)}, u32[]{:S(2)}) copy-start(f32[3,16,4096]{2,1,0:T(8,128)} %param.7) | copy-start | bytes 2359300
  0.0 27.1 %collective-permute-start.1 = (f32[3,16,4096]{2,1,0:T(8,128)}, f32[3,16,4096]{2,1,0:T(8,128)S(1)}, u32[]{:S(2)}, u32[]{:S(2)}) collective-permute-start(f32[3,16,4096]{2,1,0:T(8,128)} %param.7), channel_id=1, source_target_pairs={{8,0},{12,4},{16,8},{20,12},{24,16},{28,20},{32,24},{36,28},{40,32... | collective-permute-start | bytes 2359304 | tf_op jit(solution)/shard_map/ppermute | solution.py:22
  8.9 34.4 %collective-permute-start = (f32[3,16,4096]{2,1,0:T(8,128)}, f32[3,16,4096]{2,1,0:T(8,128)S(1)}, u32[]{:S(2)}, u32[]{:S(2)}) collective-permute-start(f32[3,16,4096]{2,1,0:T(8,128)} %param.7), channel_id=1, source_target_pairs={{4,0},{8,4},{12,8},{16,12},{20,16},{24,20},{28,24},{32,28},{36,32}... | collective-permute-start | bytes 2359304 | tf_op jit(solution)/shard_map/ppermute | solution.py:22
  74.8 1.0 copy-start.8
  81.9 17.9 %all-to-all-start.1 = ((f32[2,64,16,128]{3,2,0,1:T(8,128)}), f32[2,64,16,128]{3,2,0,1:T(8,128)S(1)}, u32[]{:S(2)}, u32[]{:S(2)}) async-start(f32[2,64,16,128]{3,2,0,1:T(8,128)} %copy.54), calls=%async_computation.1 | async-start | bytes 2097152 | tf_op jit(solution)/shard_map/while/body/eval_jaxpr/all_to_all | solution.py:74
  108.3 1.2 copy-start.5
  108.3 3.7 %copy-start.1 = (f32[9,16,4096]{2,0,1:T(8,128)S(1)}, f32[9,16,4096]{2,0,1:T(8,128)}, u32[]{:S(2)}) copy-start(f32[9,16,4096]{2,0,1:T(8,128)} %get-tuple-element.361) | copy-start | bytes 7077892 | tf_op jit(solution)/shard_map/while
  112.0 6.4 %copy-start.6 = (f32[3,16,4096]{2,0,1:T(4,128)}, f32[3,16,4096]{2,0,1:T(4,128)S(1)}, u32[]{:S(2)}) copy-start(f32[3,16,4096]{2,0,1:T(4,128)S(1)} %convolution_add_fusion.4) | copy-start | bytes 2359300 | tf_op jit(solution)/shard_map/while
  112.0 8.4 %copy-start.4 = (f32[3,16,4096]{2,1,0:T(8,128)S(1)}, f32[3,16,4096]{2,1,0:T(8,128)}, u32[]{:S(2)}) copy-start(f32[3,16,4096]{2,1,0:T(8,128)} %get-tuple-element.406) | copy-start | bytes 2359300 | tf_op jit(solution)/shard_map/while
  118.4 1.9 copy-start.2
  150.2 1.0 copy-start.8
  157.4 17.9 %all-to-all-start.1 = ((f32[2,64,16,128]{3,2,0,1:T(8,128)}), f32[2,64,16,128]{3,2,0,1:T(8,128)S(1)}, u32[]{:S(2)}, u32[]{:S(2)}) async-start(f32[2,64,16,128]{3,2,0,1:T(8,128)} %copy.54), calls=%async_computation.1 | async-start | bytes 2097152 | tf_op jit(solution)/shard_map/while/body/eval_jaxpr/all_to_all | solution.py:74
  183.7 1.2 copy-start.5
  183.7 3.7 %copy-start.1 = (f32[9,16,4096]{2,0,1:T(8,128)S(1)}, f32[9,16,4096]{2,0,1:T(8,128)}, u32[]{:S(2)}) copy-start(f32[9,16,4096]{2,0,1:T(8,128)} %get-tuple-element.361) | copy-start | bytes 7077892 | tf_op jit(solution)/shard_map/while
  187.4 6.4 %copy-start.6 = (f32[3,16,4096]{2,0,1:T(4,128)}, f32[3,16,4096]{2,0,1:T(4,128)S(1)}, u32[]{:S(2)}) copy-start(f32[3,16,4096]{2,0,1:T(4,128)S(1)} %convolution_add_fusion.4) | copy-start | bytes 2359300 | tf_op jit(solution)/shard_map/while
  187.4 8.4 %copy-start.4 = (f32[3,16,4096]{2,1,0:T(8,128)S(1)}, f32[3,16,4096]{2,1,0:T(8,128)}, u32[]{:S(2)}) copy-start(f32[3,16,4096]{2,1,0:T(8,128)} %get-tuple-element.406) | copy-start | bytes 2359300 | tf_op jit(solution)/shard_map/while
  193.9 1.9 copy-start.2
  225.6 1.0 copy-start.8
  232.8 17.9 %all-to-all-start.1 = ((f32[2,64,16,128]{3,2,0,1:T(8,128)}), f32[2,64,16,128]{3,2,0,1:T(8,128)S(1)}, u32[]{:S(2)}, u32[]{:S(2)}) async-start(f32[2,64,16,128]{3,2,0,1:T(8,128)} %copy.54), calls=%async_computation.1 | async-start | bytes 2097152 | tf_op jit(solution)/shard_map/while/body/eval_jaxpr/all_to_all | solution.py:74
  259.2 1.2 copy-start.5
  259.2 3.7 %copy-start.1 = (f32[9,16,4096]{2,0,1:T(8,128)S(1)}, f32[9,16,4096]{2,0,1:T(8,128)}, u32[]{:S(2)}) copy-start(f32[9,16,4096]{2,0,1:T(8,128)} %get-tuple-element.361) | copy-start | bytes 7077892 | tf_op jit(solution)/shard_map/while
  262.9 6.4 %copy-start.6 = (f32[3,16,4096]{2,0,1:T(4,128)}, f32[3,16,4096]{2,0,1:T(4,128)S(1)}, u32[]{:S(2)}) copy-start(f32[3,16,4096]{2,0,1:T(4,128)S(1)} %convolution_add_fusion.4) | copy-start | bytes 2359300 | tf_op jit(solution)/shard_map/while
  262.9 8.4 %copy-start.4 = (f32[3,16,4096]{2,1,0:T(8,128)S(1)}, f32[3,16,4096]{2,1,0:T(8,128)}, u32[]{:S(2)}) copy-start(f32[3,16,4096]{2,1,0:T(8,128)} %get-tuple-element.406) | copy-start | bytes 2359300 | tf_op jit(solution)/shard_map/while
  269.3 1.9 copy-start.2
  274.8 42.6 %copy-start.7 = (f32[3,16,4096]{2,0,1:T(4,128)S(1)}, f32[3,16,4096]{2,0,1:T(4,128)}, u32[]{:S(2)}) copy-start(f32[3,16,4096]{2,0,1:T(4,128)} %get-tuple-element.393) | copy-start | bytes 2359300
  274.9 25.5 %collective-permute-start.3 = (f32[3,16,4096]{2,1,0:T(8,128)S(1)}, f32[3,16,4096]{2,1,0:T(8,128)S(1)}, u32[]{:S(2)}, u32[]{:S(2)}) collective-permute-start(f32[3,16,4096]{2,1,0:T(8,128)S(1)} %get-tuple-element.227), channel_id=1, source_target_pairs={{120,0},{124,4},{0,8},{4,12},{8,16},{12,20},{16,24},{20,28},{24,32... | collective-permute-start | bytes 2359304 | tf_op jit(solution)/shard_map/ppermute | solution.py:22
  275.0 42.3 %collective-permute-start.2 = (f32[3,16,4096]{2,1,0:T(8,128)S(1)}, f32[3,16,4096]{2,1,0:T(8,128)S(1)}, u32[]{:S(2)}, u32[]{:S(2)}) collective-permute-start(f32[3,16,4096]{2,1,0:T(8,128)S(1)} %get-tuple-element.226), channel_id=1, source_target_pairs={{124,0},{0,4},{4,8},{8,12},{12,16},{16,20},{20,24},{24,28},{28,32}... | collective-permute-start | bytes 2359304 | tf_op jit(solution)/shard_map/ppermute | solution.py:22
where the time goes:
time: 320 us; the launch traced here: 319 us
  waiting for transfers between devices  107 us (33%)
  matrix products  64 us (20%)
  local copies, waits for them, and re-layouts  59.6 us (19%)
  blocking collectives  50.6 us (16%)
  starting transfers between devices  22.5 us (7%)
  other arithmetic  14.3 us (4%)
    ppermute x4, waiting for transfers between devices, shifted(): return lax.ppermute(block, axis, route)  63.8 us
    all_to_all x3, blocking collectives, solve_poisson(): lax.all_to_all(spectrum, 'grid', split_axis=2, concat_axis=1, tiled=True)  50.6 us
    all_to_all x3, waiting for transfers between devices, solve_poisson(): lax.all_to_all(columns, 'grid', split_axis=1, concat_axis=2, tiled=True)  43.1 us
    dot_general x3, matrix products, one_turn(): jnp.einsum('sq,swt->qwt', visit_onehot_mask, weighted_density * leading_o...  19.2 us
    dot_general x12, matrix products, transform_axis(): jnp.einsum(formula, cosine_table, values_in, precision=EXACT_PRECISION)  17.1 us
    dot_general x12, matrix products, transform_axis(): jnp.einsum(formula, sine_table, values_in, precision=EXACT_PRECISION)  14.2 us
    ppermute x4, starting transfers between devices, shifted(): return lax.ppermute(block, axis, route)  11.9 us
    all_to_all x3, starting transfers between devices, solve_poisson(): lax.all_to_all(columns, 'grid', split_axis=1, concat_axis=2, tiled=True)  10.5 us
  transfers between devices with their start and end apart: 7, of which 7 were waited for; matrix products, arithmetic and copies ran while one was open for 3% of the time, Pallas kernels for 0%

commit v1 on v0

--- a/solution.py
+++ b/solution.py
@@ -67,7 +67,9 @@
     joined = jnp.concatenate([cubes[0::2], cubes[1::2]], axis=-1)
     spectrum = jnp.einsum("pxyz,zk->pxyk", joined, z_tables[0], precision=EXACT_PRECISION)
     spectrum = transform_axis(spectrum, tables, "ky,pxyc->pxkc", 1.0)
-    columns = lax.all_to_all(spectrum, "grid", split_axis=2, concat_axis=1, tiled=True)
+    parts = jnp.split(spectrum, lax.axis_size("grid"), axis=2)
+    received = lax.all_to_all(jnp.stack(parts), "grid", 0, 0)
+    columns = jnp.concatenate(received, axis=1)
     columns = transform_axis(columns, tables, "kx,pxyc->pkyc", 1.0)
     columns = columns * kernel_pair[None]
     columns = transform_axis(columns, tables, "kx,pxyc->pkyc", -1.0)

time: 320 us -> 320 us (level)
    add x6 -> x3, local copies, waits for them, and re-layouts: 6.53 us -> 4.73 us  [transform_axis(): return direct_part + sweep_direction * rotate_parts(crossed_part)]
where the time goes in v1:
time: 320 us; the launch traced here: 319 us
  waiting for transfers between devices  107 us (33%)
  matrix products  65.4 us (20%)
  local copies, waits for them, and re-layouts  57.9 us (18%)
  blocking collectives  50.6 us (16%)
  starting transfers between devices  22.5 us (7%)
  other arithmetic  14.5 us (5%)
    ppermute x4, waiting for transfers between devices, shifted(): return lax.ppermute(block, axis, route)  63.8 us
    all_to_all x3, blocking collectives, solve_poisson(): received = lax.all_to_all(jnp.stack(parts), 'grid', 0, 0)  50.6 us
    all_to_all x3, waiting for transfers between devices, solve_poisson(): lax.all_to_all(columns, 'grid', split_axis=1, concat_axis=2, tiled=True)  43.1 us
    dot_general x3, matrix products, one_turn(): jnp.einsum('sq,swt->qwt', visit_onehot_mask, weighted_density * leading_o...  19.2 us
    dot_general x12, matrix products, transform_axis(): jnp.einsum(formula, cosine_table, values_in, precision=EXACT_PRECISION)  17.8 us
    dot_general x12, matrix products, transform_axis(): jnp.einsum(formula, sine_table, values_in, precision=EXACT_PRECISION)  14.9 us
    ppermute x4, starting transfers between devices, shifted(): return lax.ppermute(block, axis, route)  11.9 us
    all_to_all x3, starting transfers between devices, solve_poisson(): lax.all_to_all(columns, 'grid', split_axis=1, concat_axis=2, tiled=True)  10.5 us
  transfers between devices with their start and end apart: 7, of which 7 were waited for; matrix products, arithmetic and copies ran while one was open for 3% of the time, Pallas kernels for 0%

profile of v1, /device:TPU:0, one launch (start us, length us, event | category | flops | bytes accessed | tf_op | source)
XLA Modules:
  0.0 318.8 jit_solution(9582572326664614585)
XLA Ops:
  0.0 8.9 %collective-permute-start.1 = (f32[3,16,4096]{2,1,0:T(8,128)}, f32[3,16,4096]{2,1,0:T(8,128)S(1)}, u32[]{:S(2)}, u32[]{:S(2)}) collective-permute-start(f32[3,16,4096]{2,1,0:T(8,128)} %param.7), channel_id=1, source_target_pairs={{8,0},{12,4},{16,8},{20,12},{24,16},{28,20},{32,24},{36,28},{40,32... | collective-permute-start | bytes 2359304 | tf_op jit(solution)/shard_map/ppermute | solution.py:22
  11.1 1.6 sort.17
  19.6 7.6 %collective-permute-done.1 = f32[3,16,4096]{2,1,0:T(8,128)S(1)} collective-permute-done((f32[3,16,4096]{2,1,0:T(8,128)}, f32[3,16,4096]{2,1,0:T(8,128)S(1)}, u32[]{:S(2)}, u32[]{:S(2)}) %collective-permute-start.1) | collective-permute-done | bytes 786464 | tf_op jit(solution)/shard_map/ppermute | solution.py:22
  27.2 16.1 %collective-permute-done = f32[3,16,4096]{2,1,0:T(8,128)S(1)} collective-permute-done((f32[3,16,4096]{2,1,0:T(8,128)}, f32[3,16,4096]{2,1,0:T(8,128)S(1)}, u32[]{:S(2)}, u32[]{:S(2)}) %collective-permute-start) | collective-permute-done | bytes 786464 | tf_op jit(solution)/shard_map/ppermute | solution.py:22
  43.3 1.7 pad_maximum_fusion.2
  44.9 226.3 %while.14 = (s32[]{:T(128)}, f32[3,16,4096]{2,0,1:T(4,128)}, f32[9,16,4096]{2,0,1:T(8,128)}, s32[3,4]{1,0:T(4,128)S(1)}, f32[3,16,4096]{2,1,0:T(8,128)S(1)}, /*i...) while((s32[]{:T(128)}, f32[3,16,4096]{2,0,1:T(4,128)}, ...), condition=%wide.region_2.3_spmd.clone.clone, body=%wide.region_1.2_spmd.clone.clone.sunk | while | flops 2461468672 | bytes 113910440 | solution.py:170
  45.6 2.3 gather_fusion.1
  48.0 2.2 mul.862
  50.2 1.7 fusion.196
  56.2 16.9 %all_to_all.32 = f32[4,2,16,16,128]{4,3,2,1,0:T(8,128)S(1)} all-to-all(f32[4,2,16,16,128]{4,3,2,1,0:T(8,128)S(1)} %pad_maximum_fusion.10), channel_id=1, replica_groups=mesh['band'=32,'grid'=4] {'grid'}, dimensions={0} | all-to-all | bytes 2097152 | tf_op jit(solution)/shard_map/while/body/eval_jaxpr/all_to_all | solution.py:71
  75.6 1.8 fusion.201
  80.4 1.6 copy.62
  81.9 3.5 %all-to-all-start.1 = ((f32[2,64,16,128]{3,2,0,1:T(8,128)}), f32[2,64,16,128]{3,2,0,1:T(8,128)S(1)}, u32[]{:S(2)}, u32[]{:S(2)}) async-start(f32[2,64,16,128]{3,2,0,1:T(8,128)} %copy.62), calls=%async_computation.1 | async-start | bytes 2097152 | tf_op jit(solution)/shard_map/while/body/eval_jaxpr/all_to_all | solution.py:76
  85.5 14.4 %all-to-all-done.1 = f32[2,64,16,128]{3,2,0,1:T(8,128)S(1)} async-done(((f32[2,64,16,128]{3,2,0,1:T(8,128)}), f32[2,64,16,128]{3,2,0,1:T(8,128)S(1)}, u32[]{:S(2)}, u32[]{:S(2)}) %all-to-all-start.1) | async-done | bytes 1048608 | tf_op jit(solution)/shard_map/while/body/eval_jaxpr/all_to_all | solution.py:76
  104.6 1.5 copy.64
  106.2 2.1 reshape.265
  109.5 2.5 convolution_add_fusion.4
  112.0 6.4 %convolution_add_fusion.5 = f32[9,16,4096]{2,0,1:T(8,128)S(1)} fusion(f32[9,16,4096]{2,0,1:T(8,128)S(1)} %copy-done.1, pred[]{:T(512)S(6)} %compare.9, f32[4,16,4096]{2,1,0:T(8,128)S(1)} %get-tuple-element.354, f32[4]{0:T(128)S(1)} %get-tuple-element.355, s32[4]{0:T(128)S(1)} %get-tuple-element.356), kind=kOutput, calls=%fused_computation.9.clone.1 | convolution fusion | flops 29491272 | bytes 5767201 | tf_op jit(solution)/shard_map/while/body/eval_jaxpr/sq,swt->qwt/dot_general | solution.py:152
  118.4 1.9 copy-done.2
  121.0 2.3 gather_fusion.1
  123.4 2.2 mul.862
  125.6 1.7 fusion.196
  131.6 16.9 %all_to_all.32 = f32[4,2,16,16,128]{4,3,2,1,0:T(8,128)S(1)} all-to-all(f32[4,2,16,16,128]{4,3,2,1,0:T(8,128)S(1)} %pad_maximum_fusion.10), channel_id=1, replica_groups=mesh['band'=32,'grid'=4] {'grid'}, dimensions={0} | all-to-all | bytes 2097152 | tf_op jit(solution)/shard_map/while/body/eval_jaxpr/all_to_all | solution.py:71
  151.0 1.8 fusion.201
  155.8 1.6 copy.62
  157.4 3.5 %all-to-all-start.1 = ((f32[2,64,16,128]{3,2,0,1:T(8,128)}), f32[2,64,16,128]{3,2,0,1:T(8,128)S(1)}, u32[]{:S(2)}, u32[]{:S(2)}) async-start(f32[2,64,16,128]{3,2,0,1:T(8,128)} %copy.62), calls=%async_computation.1 | async-start | bytes 2097152 | tf_op jit(solution)/shard_map/while/body/eval_jaxpr/all_to_all | solution.py:76
  160.9 14.4 %all-to-all-done.1 = f32[2,64,16,128]{3,2,0,1:T(8,128)S(1)} async-done(((f32[2,64,16,128]{3,2,0,1:T(8,128)}), f32[2,64,16,128]{3,2,0,1:T(8,128)S(1)}, u32[]{:S(2)}, u32[]{:S(2)}) %all-to-all-start.1) | async-done | bytes 1048608 | tf_op jit(solution)/shard_map/while/body/eval_jaxpr/all_to_all | solution.py:76
  181.6 2.1 reshape.265
  185.0 2.5 convolution_add_fusion.4
  187.4 6.4 %convolution_add_fusion.5 = f32[9,16,4096]{2,0,1:T(8,128)S(1)} fusion(f32[9,16,4096]{2,0,1:T(8,128)S(1)} %copy-done.1, pred[]{:T(512)S(6)} %compare.9, f32[4,16,4096]{2,1,0:T(8,128)S(1)} %get-tuple-element.354, f32[4]{0:T(128)S(1)} %get-tuple-element.355, s32[4]{0:T(128)S(1)} %get-tuple-element.356), kind=kOutput, calls=%fused_computation.9.clone.1 | convolution fusion | flops 29491272 | bytes 5767201 | tf_op jit(solution)/shard_map/while/body/eval_jaxpr/sq,swt->qwt/dot_general | solution.py:152
  193.9 1.9 copy-done.2
  196.4 2.3 gather_fusion.1
  198.9 2.2 mul.862
  201.1 1.7 fusion.196
  207.0 16.9 %all_to_all.32 = f32[4,2,16,16,128]{4,3,2,1,0:T(8,128)S(1)} all-to-all(f32[4,2,16,16,128]{4,3,2,1,0:T(8,128)S(1)} %pad_maximum_fusion.10), channel_id=1, replica_groups=mesh['band'=32,'grid'=4] {'grid'}, dimensions={0} | all-to-all | bytes 2097152 | tf_op jit(solution)/shard_map/while/body/eval_jaxpr/all_to_all | solution.py:71
  226.5 1.8 fusion.201
  231.2 1.6 copy.62
  232.8 3.5 %all-to-all-start.1 = ((f32[2,64,16,128]{3,2,0,1:T(8,128)}), f32[2,64,16,128]{3,2,0,1:T(8,128)S(1)}, u32[]{:S(2)}, u32[]{:S(2)}) async-start(f32[2,64,16,128]{3,2,0,1:T(8,128)} %copy.62), calls=%async_computation.1 | async-start | bytes 2097152 | tf_op jit(solution)/shard_map/while/body/eval_jaxpr/all_to_all | solution.py:76
  236.4 14.4 %all-to-all-done.1 = f32[2,64,16,128]{3,2,0,1:T(8,128)S(1)} async-done(((f32[2,64,16,128]{3,2,0,1:T(8,128)}), f32[2,64,16,128]{3,2,0,1:T(8,128)S(1)}, u32[]{:S(2)}, u32[]{:S(2)}) %all-to-all-start.1) | async-done | bytes 1048608 | tf_op jit(solution)/shard_map/while/body/eval_jaxpr/all_to_all | solution.py:76
  255.5 1.5 copy.64
  257.0 2.1 reshape.265
  260.4 2.5 convolution_add_fusion.4
  262.9 6.4 %convolution_add_fusion.5 = f32[9,16,4096]{2,0,1:T(8,128)S(1)} fusion(f32[9,16,4096]{2,0,1:T(8,128)S(1)} %copy-done.1, pred[]{:T(512)S(6)} %compare.9, f32[4,16,4096]{2,1,0:T(8,128)S(1)} %get-tuple-element.354, f32[4]{0:T(128)S(1)} %get-tuple-element.355, s32[4]{0:T(128)S(1)} %get-tuple-element.356), kind=kOutput, calls=%fused_computation.9.clone.1 | convolution fusion | flops 29491272 | bytes 5767201 | tf_op jit(solution)/shard_map/while/body/eval_jaxpr/sq,swt->qwt/dot_general | solution.py:152
  269.3 1.9 copy-done.2
  271.2 3.6 %copy.32 = f32[9,16,4096]{2,1,0:T(8,128)S(1)} copy(f32[9,16,4096]{2,0,1:T(8,128)} %get-tuple-element.406) | data formatting | bytes 4718592 | tf_op jit(solution)/shard_map/while | solution.py:170
  275.0 2.2 collective-permute-start.2
  277.2 23.2 %collective-permute-done.3 = f32[3,16,4096]{2,1,0:T(8,128)S(1)} collective-permute-done((f32[3,16,4096]{2,1,0:T(8,128)S(1)}, f32[3,16,4096]{2,1,0:T(8,128)S(1)}, u32[]{:S(2)}, u32[]{:S(2)}) %collective-permute-start.3) | collective-permute-done | bytes 786464 | tf_op jit(solution)/shard_map/ppermute | solution.py:22
  300.4 16.9 %collective-permute-done.2 = f32[3,16,4096]{2,1,0:T(8,128)S(1)} collective-permute-done((f32[3,16,4096]{2,1,0:T(8,128)S(1)}, f32[3,16,4096]{2,1,0:T(8,128)S(1)}, u32[]{:S(2)}, u32[]{:S(2)}) %collective-permute-start.2) | collective-permute-done | bytes 786464 | tf_op jit(solution)/shard_map/ppermute | solution.py:22
  (155 shorter events, 61.5 us)
Async XLA Ops:
  0.0 10.3 %copy-start = (s32[96,96]{1,0:T(8,128)S(1)}, s32[96,96]{1,0:T(8,128)}, u32[]{:S(2)}) copy-start(s32[96,96]{1,0:T(8,128)} %param.8) | copy-start | bytes 110596
  0.0 43.3 %copy-start.3 = (f32[3,16,4096]{2,1,0:T(8,128)S(1)}, f32[3,16,4096]{2,1,0:T(8,128)}, u32[]{:S(2)}) copy-start(f32[3,16,4096]{2,1,0:T(8,128)} %param.7) | copy-start | bytes 2359300
  0.0 27.1 %collective-permute-start.1 = (f32[3,16,4096]{2,1,0:T(8,128)}, f32[3,16,4096]{2,1,0:T(8,128)S(1)}, u32[]{:S(2)}, u32[]{:S(2)}) collective-permute-start(f32[3,16,4096]{2,1,0:T(8,128)} %param.7), channel_id=1, source_target_pairs={{8,0},{12,4},{16,8},{20,12},{24,16},{28,20},{32,24},{36,28},{40,32... | collective-permute-start | bytes 2359304 | tf_op jit(solution)/shard_map/ppermute | solution.py:22
  8.9 34.4 %collective-permute-start = (f32[3,16,4096]{2,1,0:T(8,128)}, f32[3,16,4096]{2,1,0:T(8,128)S(1)}, u32[]{:S(2)}, u32[]{:S(2)}) collective-permute-start(f32[3,16,4096]{2,1,0:T(8,128)} %param.7), channel_id=1, source_target_pairs={{4,0},{8,4},{12,8},{16,12},{20,16},{24,20},{28,24},{32,28},{36,32}... | collective-permute-start | bytes 2359304 | tf_op jit(solution)/shard_map/ppermute | solution.py:22
  74.5 1.0 copy-start.8
  81.9 17.9 %all-to-all-start.1 = ((f32[2,64,16,128]{3,2,0,1:T(8,128)}), f32[2,64,16,128]{3,2,0,1:T(8,128)S(1)}, u32[]{:S(2)}, u32[]{:S(2)}) async-start(f32[2,64,16,128]{3,2,0,1:T(8,128)} %copy.62), calls=%async_computation.1 | async-start | bytes 2097152 | tf_op jit(solution)/shard_map/while/body/eval_jaxpr/all_to_all | solution.py:76
  108.3 1.2 copy-start.5
  108.3 3.7 %copy-start.1 = (f32[9,16,4096]{2,0,1:T(8,128)S(1)}, f32[9,16,4096]{2,0,1:T(8,128)}, u32[]{:S(2)}) copy-start(f32[9,16,4096]{2,0,1:T(8,128)} %get-tuple-element.373) | copy-start | bytes 7077892 | tf_op jit(solution)/shard_map/while
  112.0 6.4 %copy-start.6 = (f32[3,16,4096]{2,0,1:T(4,128)}, f32[3,16,4096]{2,0,1:T(4,128)S(1)}, u32[]{:S(2)}) copy-start(f32[3,16,4096]{2,0,1:T(4,128)S(1)} %convolution_add_fusion.4) | copy-start | bytes 2359300 | tf_op jit(solution)/shard_map/while
  112.0 8.4 %copy-start.4 = (f32[3,16,4096]{2,1,0:T(8,128)S(1)}, f32[3,16,4096]{2,1,0:T(8,128)}, u32[]{:S(2)}) copy-start(f32[3,16,4096]{2,1,0:T(8,128)} %get-tuple-element.418) | copy-start | bytes 2359300 | tf_op jit(solution)/shard_map/while
  118.4 1.9 copy-start.2
  150.0 1.0 copy-start.8
  157.4 17.9 %all-to-all-start.1 = ((f32[2,64,16,128]{3,2,0,1:T(8,128)}), f32[2,64,16,128]{3,2,0,1:T(8,128)S(1)}, u32[]{:S(2)}, u32[]{:S(2)}) async-start(f32[2,64,16,128]{3,2,0,1:T(8,128)} %copy.62), calls=%async_computation.1 | async-start | bytes 2097152 | tf_op jit(solution)/shard_map/while/body/eval_jaxpr/all_to_all | solution.py:76
  183.7 1.2 copy-start.5
  183.7 3.7 %copy-start.1 = (f32[9,16,4096]{2,0,1:T(8,128)S(1)}, f32[9,16,4096]{2,0,1:T(8,128)}, u32[]{:S(2)}) copy-start(f32[9,16,4096]{2,0,1:T(8,128)} %get-tuple-element.373) | copy-start | bytes 7077892 | tf_op jit(solution)/shard_map/while
  187.4 6.4 %copy-start.6 = (f32[3,16,4096]{2,0,1:T(4,128)}, f32[3,16,4096]{2,0,1:T(4,128)S(1)}, u32[]{:S(2)}) copy-start(f32[3,16,4096]{2,0,1:T(4,128)S(1)} %convolution_add_fusion.4) | copy-start | bytes 2359300 | tf_op jit(solution)/shard_map/while
  187.4 8.4 %copy-start.4 = (f32[3,16,4096]{2,1,0:T(8,128)S(1)}, f32[3,16,4096]{2,1,0:T(8,128)}, u32[]{:S(2)}) copy-start(f32[3,16,4096]{2,1,0:T(8,128)} %get-tuple-element.418) | copy-start | bytes 2359300 | tf_op jit(solution)/shard_map/while
  193.8 1.9 copy-start.2
  225.4 1.0 copy-start.8
  232.8 17.9 %all-to-all-start.1 = ((f32[2,64,16,128]{3,2,0,1:T(8,128)}), f32[2,64,16,128]{3,2,0,1:T(8,128)S(1)}, u32[]{:S(2)}, u32[]{:S(2)}) async-start(f32[2,64,16,128]{3,2,0,1:T(8,128)} %copy.62), calls=%async_computation.1 | async-start | bytes 2097152 | tf_op jit(solution)/shard_map/while/body/eval_jaxpr/all_to_all | solution.py:76
  259.2 1.2 copy-start.5
  259.2 3.7 %copy-start.1 = (f32[9,16,4096]{2,0,1:T(8,128)S(1)}, f32[9,16,4096]{2,0,1:T(8,128)}, u32[]{:S(2)}) copy-start(f32[9,16,4096]{2,0,1:T(8,128)} %get-tuple-element.373) | copy-start | bytes 7077892 | tf_op jit(solution)/shard_map/while
  262.9 6.4 %copy-start.6 = (f32[3,16,4096]{2,0,1:T(4,128)}, f32[3,16,4096]{2,0,1:T(4,128)S(1)}, u32[]{:S(2)}) copy-start(f32[3,16,4096]{2,0,1:T(4,128)S(1)} %convolution_add_fusion.4) | copy-start | bytes 2359300 | tf_op jit(solution)/shard_map/while
  262.9 8.4 %copy-start.4 = (f32[3,16,4096]{2,1,0:T(8,128)S(1)}, f32[3,16,4096]{2,1,0:T(8,128)}, u32[]{:S(2)}) copy-start(f32[3,16,4096]{2,1,0:T(8,128)} %get-tuple-element.418) | copy-start | bytes 2359300 | tf_op jit(solution)/shard_map/while
  269.3 1.9 copy-start.2
  274.8 42.6 %copy-start.7 = (f32[3,16,4096]{2,0,1:T(4,128)S(1)}, f32[3,16,4096]{2,0,1:T(4,128)}, u32[]{:S(2)}) copy-start(f32[3,16,4096]{2,0,1:T(4,128)} %get-tuple-element.405) | copy-start | bytes 2359300
  274.9 25.5 %collective-permute-start.3 = (f32[3,16,4096]{2,1,0:T(8,128)S(1)}, f32[3,16,4096]{2,1,0:T(8,128)S(1)}, u32[]{:S(2)}, u32[]{:S(2)}) collective-permute-start(f32[3,16,4096]{2,1,0:T(8,128)S(1)} %get-tuple-element.231), channel_id=1, source_target_pairs={{120,0},{124,4},{0,8},{4,12},{8,16},{12,20},{16,24},{20,28},{24,32... | collective-permute-start | bytes 2359304 | tf_op jit(solution)/shard_map/ppermute | solution.py:22
  275.0 42.3 %collective-permute-start.2 = (f32[3,16,4096]{2,1,0:T(8,128)S(1)}, f32[3,16,4096]{2,1,0:T(8,128)S(1)}, u32[]{:S(2)}, u32[]{:S(2)}) collective-permute-start(f32[3,16,4096]{2,1,0:T(8,128)S(1)} %get-tuple-element.230), channel_id=1, source_target_pairs={{124,0},{0,4},{4,8},{8,12},{12,16},{16,20},{20,24},{24,28},{28,32}... | collective-permute-start | bytes 2359304 | tf_op jit(solution)/shard_map/ppermute | solution.py:22
